TPU v7x, 256 devices: a whole 4x4x8 slice. The times are simulated.
256 devices in a mesh: dp: 2 (over core), ret: 16 (over y, x), ctx: 8 (over z).
Axes of the slice: x: 4, y: 4, z: 8, core: 2. Of those that a mesh axis runs over, the one named last changes fastest.
Arguments:
- queries: bfloat16 [2, 8192, 4096], P('dp', 'ret', 'ctx'), may hold values from -6 to 6
- enc_states: bfloat16 [2, 32768, 896], P('dp', 'ret'), may hold values from -1600 to 1600
- w_key: bfloat16 [896, 4096], P(None, 'ctx'), may hold values from -0.1875 to 0.1875
- w_value: bfloat16 [896, 4096], P(None, 'ctx'), may hold values from -0.59765625 to 0.59765625
- shard_ids: int32 [2, 128, 2], P('dp', 'ret'), may hold values from 0 to 15, all different within a row; in each aligned block of 8 rows (0 to 7, 8 to 15, ..., all dimensions but the last counted through in order) at most 2 rows name the same one
- row_ids: int32 [2, 128, 2], P('dp', 'ret'), may hold values from 0 to 15
- grad_out: bfloat16 [2, 8192, 4096], P('dp', 'ret', 'ctx'), may hold values from -6 to 6
Outputs:
- attended: bfloat16 [2, 8192, 4096], P('dp', 'ret', 'ctx')
- grad_queries: bfloat16 [2, 8192, 4096], P('dp', 'ret', 'ctx')
- grad_w_key: float32 [896, 4096], P(('dp', 'ret'), 'ctx')
- grad_w_value: float32 [896, 4096], P(('dp', 'ret'), 'ctx')
Inputs may be any that keep to these rules, and one draw needn't show every extreme that they name: `shard_ids`: each block names 2 different shards; among the 8 blocks that one index of ret holds, no shard is named by more than 2 blocks, a bound that some block reaches.
All inputs are finite; a program needn't handle non-finite values.
Results may differ from a plain program's by a relative error of at most 0.019.
Values may be sent and summed in bfloat16 or wider, within the bound.
A program may use at most 128 MiB of HBM per device.

v0:
```python
import math
import jax
import jax.numpy as jnp
from jax import lax
from jax.sharding import PartitionSpec as P

HEAD_DIM = 128
NEIGH_LEN = 128
NEIGHBOURS = 2


def normalize_rows(states):
    floats = states.astype(jnp.float32)
    mean_square = jnp.mean(floats * floats, axis=-1, keepdims=True)
    return (floats * lax.rsqrt(mean_square + 1e-06)).astype(jnp.bfloat16)


def contract_rows(lhs_rows, rhs_rows):
    return lax.dot_general(
        lhs_rows, rhs_rows, (((0,), (0,)), ((), ())), preferred_element_type=jnp.float32
    )


def attend(query_block, key_block, value_block, grad_block):
    score_scale = 1.0 / math.sqrt(HEAD_DIM)
    scores = (
        jnp.einsum("cthd,cjhd->chtj", query_block, key_block, preferred_element_type=jnp.float32)
        * score_scale
    )
    exponent = jnp.exp(scores)
    denominator = jnp.sum(exponent, axis=-1)
    numerator = jnp.einsum(
        "chtj,cjhd->cthd",
        exponent.astype(jnp.bfloat16),
        value_block,
        preferred_element_type=jnp.float32,
    )
    output = numerator / jnp.transpose(denominator, (0, 2, 1))[..., None]
    prob_grad = jnp.einsum(
        "cthd,cjhd->chtj", grad_block, value_block, preferred_element_type=jnp.float32
    )
    row_delta = jnp.transpose(jnp.sum(grad_block.astype(jnp.float32) * output, axis=-1), (0, 2, 1))
    probability = exponent / denominator[..., None]
    score_grad = (probability * (prob_grad - row_delta[..., None]) * score_scale).astype(
        jnp.bfloat16
    )
    grad_query = jnp.einsum(
        "chtj,cjhd->cthd", score_grad, key_block, preferred_element_type=jnp.float32
    ).astype(jnp.bfloat16)
    grad_key = jnp.einsum(
        "chtj,cthd->cjhd", score_grad, query_block, preferred_element_type=jnp.float32
    ).astype(jnp.bfloat16)
    grad_value = jnp.einsum(
        "chtj,cthd->cjhd",
        probability.astype(jnp.bfloat16),
        grad_block,
        preferred_element_type=jnp.float32,
    ).astype(jnp.bfloat16)
    return (output.astype(jnp.bfloat16), grad_query, grad_key, grad_value)


def local(queries, enc_states, w_key, w_value, shard_ids, row_ids, grad_out):
    n_ret = lax.axis_size("ret")
    me_index = lax.axis_index("ret")
    blocks = shard_ids.shape[1]
    request_count = blocks * NEIGHBOURS
    capacity = request_count * 2 // n_ret
    feat_width = queries.shape[2]
    head_count = feat_width // HEAD_DIM
    db_dev = enc_states.shape[1] // NEIGH_LEN
    enc_width = enc_states.shape[2]
    context_rows = NEIGHBOURS * NEIGH_LEN
    every_shard, every_row = (
        lax.all_gather(shard_ids, "ret", axis=1, tiled=True),
        lax.all_gather(row_ids, "ret", axis=1, tiled=True),
    )
    req_shard = every_shard.reshape(n_ret, request_count)
    req_row = every_row.reshape(n_ret, request_count)
    positions = jnp.arange(request_count, dtype=jnp.int32)
    earlier = positions[None, :] < positions[:, None]
    same_shard = req_shard[:, :, None] == req_shard[:, None, :]
    slot_rank = jnp.sum((same_shard & earlier[None]).astype(jnp.int32), axis=2)
    own_shard = shard_ids.reshape(request_count)
    own_same = own_shard[:, None] == own_shard[None, :]
    own_rank = jnp.sum((own_same & earlier).astype(jnp.int32), axis=1)
    own_slot = own_shard * capacity + own_rank
    slot_iota = jnp.arange(capacity, dtype=jnp.int32)
    select = (req_shard[:, None, :] == me_index) & (
        slot_rank[:, None, :] == slot_iota[None, :, None]
    )
    filled = jnp.any(select, axis=2).reshape(-1)
    row_for = jnp.sum(jnp.where(select, req_row[:, None, :], 0), axis=2).reshape(-1)
    normed = normalize_rows(enc_states[0])
    normed_rows = normed.reshape(db_dev, NEIGH_LEN, enc_width)
    query_blocks = queries[0].reshape(blocks, -1, head_count, HEAD_DIM)
    grad_blocks = grad_out[0].reshape(blocks, -1, head_count, HEAD_DIM)
    both_weights = jnp.concatenate([w_key, w_value], axis=1)
    projected = jnp.dot(normed, both_weights, preferred_element_type=jnp.float32).astype(
        jnp.bfloat16
    )
    kv_table = projected.reshape(db_dev, NEIGH_LEN, 2 * feat_width)
    picked = jnp.take(kv_table, row_for, axis=0)
    outgoing = jnp.where(filled[:, None, None], picked, jnp.zeros_like(picked))
    outgoing = outgoing.reshape(n_ret, capacity, NEIGH_LEN, 2 * feat_width)
    incoming = lax.all_to_all(outgoing, "ret", split_axis=0, concat_axis=0, tiled=True)
    own_rows = jnp.take(
        incoming.reshape(n_ret * capacity, NEIGH_LEN, 2 * feat_width), own_slot, axis=0
    )
    own_rows = own_rows.reshape(blocks, context_rows, 2, head_count, HEAD_DIM)
    attended, grad_query, grad_key, grad_value = attend(
        query_blocks, own_rows[:, :, 0], own_rows[:, :, 1], grad_blocks
    )
    returned_grads = jnp.concatenate(
        [
            grad_key.reshape(request_count, NEIGH_LEN, feat_width),
            grad_value.reshape(request_count, NEIGH_LEN, feat_width),
        ],
        axis=2,
    )
    grad_slots = jnp.zeros((n_ret * capacity, NEIGH_LEN, 2 * feat_width), jnp.bfloat16)
    grad_slots = grad_slots.at[own_slot].set(returned_grads)
    arrived = lax.all_to_all(
        grad_slots.reshape(n_ret, capacity, NEIGH_LEN, 2 * feat_width),
        "ret",
        split_axis=0,
        concat_axis=0,
        tiled=True,
    )
    state_rows = jnp.take(normed_rows, row_for, axis=0)
    partial_value = contract_rows(
        state_rows.reshape(-1, enc_width), arrived.reshape(-1, 2 * feat_width)
    )
    summed = lax.psum_scatter(
        partial_value.astype(jnp.bfloat16), ("dp", "ret"), scatter_dimension=0, tiled=True
    ).astype(jnp.float32)
    grad_w_key = summed[:, :feat_width]
    grad_w_value = summed[:, feat_width:]
    return (
        attended.reshape(1, -1, feat_width),
        grad_query.reshape(1, -1, feat_width),
        grad_w_key,
        grad_w_value,
    )


def solution(mesh):
    placed = (
        P("dp", "ret", "ctx"),
        P("dp", "ret", None),
        P(None, "ctx"),
        P(None, "ctx"),
        P("dp", "ret", None),
        P("dp", "ret", None),
        P("dp", "ret", "ctx"),
    )
    return jax.shard_map(
        local,
        mesh=mesh,
        in_specs=placed,
        out_specs=(
            P("dp", "ret", "ctx"),
            P("dp", "ret", "ctx"),
            P(("dp", "ret"), "ctx"),
            P(("dp", "ret"), "ctx"),
        ),
        check_vma=False,
    )
```

profile of v0, /device:TPU:76, one launch (start us, length us, event | category | flops | bytes accessed | tf_op | source)
XLA Modules:
  0.0 476.9 jit_solution(10908282372569557570)
XLA Ops:
  0.7 0.9 copy.67
  1.6 22.1 %all_gather.6 = s32[1,128,2]{2,0,1:T(1,128)S(1)} all-gather(s32[1,8,2]{2,0,1:T(1,128)S(1)} %copy.67), channel_id=1, replica_groups=mesh['dp'=2,'ret'=16,'ctx'=8] {'ret'}, dimensions={1}, use_global_device_ids=true | all-gather | bytes 1088 | tf_op jit(solution)/shard_map/all_gather | solution.py:74
  23.6 0.5 broadcast.197
  24.1 0.8 reduce.7
  25.0 0.4 convert_reduce_fusion
  25.5 0.8 copy.69
  26.2 21.5 %all_gather.7 = s32[1,128,2]{2,0,1:T(1,128)S(1)} all-gather(s32[1,8,2]{2,0,1:T(1,128)S(1)} %copy.69), channel_id=1, replica_groups=mesh['dp'=2,'ret'=16,'ctx'=8] {'ret'}, dimensions={1}, use_global_device_ids=true | all-gather | bytes 1088 | tf_op jit(solution)/shard_map/all_gather | solution.py:75
  47.7 0.8 reduce.6
  49.1 2.8 fusion.1
  52.1 8.4 %convolution_convert_fusion = bf16[2048,1024]{1,0:T(8,128)(2,1)} fusion(bf16[1,2048,896]{2,1,0:T(8,128)(2,1)} %param.8, f32[2048]{0:T(1024)S(1)} %get-tuple-element.9, bf16[896,512]{1,0:T(8,128)(2,1)S(1)} %copy-done.8, bf16[896,512]{1,0:T(8,128)(2,1)S(1)} %copy-done.9), kind=kOutput, calls=%fused_computation.13 | convolution fusion | flops 3769368576 | bytes 9707520 | tf_op jit(solution)/shard_map/dot_general | solution.py:98
  60.6 7.1 %gather_fusion = bf16[32,128,1024]{2,1,0:T(8,128)(2,1)} fusion(bf16[16,128,1024]{2,1,0:T(8,128)(2,1)} %bitcast.112, s32[1024]{0:T(1024)S(1)} %pad_clamp_fusion.1), kind=kCustom, calls=%fused_computation | custom fusion | bytes 16777344 | tf_op jit(solution)/shard_map/jit(_take)/gather | solution.py:102
  67.6 7.6 %select_select_fusion = bf16[16,2,128,1024]{3,2,1,0:T(8,128)(2,1)} fusion(bf16[16,2,128,1024]{3,2,1,0:T(8,128)(2,1)} %bitcast.111, pred[16,2]{1,0:T(8,128)(4,1)S(1)} %copy.70, pred[16,2]{1,0:T(8,128)(4,1)S(1)} %copy.68), kind=kLoop, calls=%fused_computation.4 | loop fusion | flops 8388608 | bytes 16777280 | tf_op jit(solution)/shard_map/jit(_where)/select_n | solution.py:103
  75.2 8.5 %all-to-all-start = ((bf16[16,2,128,1024]{3,2,1,0:T(8,128)(2,1)}), bf16[16,2,128,1024]{3,2,1,0:T(8,128)(2,1)}, u32[]{:S(2)}, u32[]{:S(2)}) async-start(bf16[16,2,128,1024]{3,2,1,0:T(8,128)(2,1)} %select_select_fusion), calls=%async_computation | async-start | bytes 16777216 | tf_op jit(solution)/shard_map/all_to_all | solution.py:105
  84.8 90.6 %all-to-all-done = bf16[16,2,128,1024]{3,2,1,0:T(8,128)(2,1)} async-done(((bf16[16,2,128,1024]{3,2,1,0:T(8,128)(2,1)}), bf16[16,2,128,1024]{3,2,1,0:T(8,128)(2,1)}, u32[]{:S(2)}, u32[]{:S(2)}) %all-to-all-start) | async-done | bytes 8388640 | tf_op jit(solution)/shard_map/all_to_all | solution.py:105
  175.3 6.2 %gather_fusion.1 = bf16[16,128,1024]{2,1,0:T(8,128)(2,1)} fusion(bf16[32,128,1024]{2,1,0:T(8,128)(2,1)} %bitcast.6, s32[1024]{0:T(1024)S(1)} %pad_clamp_fusion), kind=kCustom, calls=%fused_computation.1 | custom fusion | bytes 8388672 | tf_op jit(solution)/shard_map/jit(_take)/gather | solution.py:106
  181.5 7.7 %reshape.255 = bf16[8,256,2,4,128]{4,3,2,1,0:T(4,128)(2,1)} reshape(bf16[16,128,1024]{2,1,0:T(8,128)(2,1)} %gather_fusion.1) | data formatting | bytes 8388608 | tf_op jit(solution)/shard_map/jit(_take)/gather | solution.py:106
  189.2 2.9 copy_select_fusion
  192.1 0.9 bitcast_reduce_fusion
  193.1 2.5 convert_bitcast_fusion
  195.6 1.5 multiply_reduce_fusion
  197.1 1.0 fusion.7
  198.2 0.8 convert_bitcast_fusion.1
  198.9 2.9 copy.82
  201.8 4.1 reshape.217
  205.9 3.3 copy.84
  209.3 2.2 reshape.218
  211.5 4.5 pad_maximum_fusion
  216.0 6.7 %copy.85 = bf16[16,128,1024]{2,1,0:T(8,128)(2,1)} copy(bf16[16,128,1024]{1,0,2:T(8,128)(2,1)} %pad_maximum_fusion) | data formatting | bytes 8388608 | tf_op jit(solution)/shard_map/concatenate | solution.py:113
  222.7 4.3 broadcast.174
  227.0 10.9 %scatter_fusion = bf16[32,128,1024]{2,1,0:T(8,128)(2,1)} fusion(bf16[32,128,1024]{2,1,0:T(8,128)(2,1)} %broadcast.174, s32[16]{0:T(128)S(1)} %fusion.27, bf16[16,128,1024]{2,1,0:T(8,128)(2,1)} %copy.85), kind=kCustom, calls=%fused_computation.3 | custom fusion | bytes 12582976 | tf_op jit(solution)/shard_map/scatter | solution.py:121
  237.8 9.6 %all-to-all-start.1 = ((bf16[16,2,128,1024]{3,2,1,0:T(8,128)(2,1)}), bf16[16,2,128,1024]{3,2,1,0:T(8,128)(2,1)}, u32[]{:S(2)}, u32[]{:S(2)}) async-start(bf16[16,2,128,1024]{3,2,1,0:T(8,128)(2,1)} %bitcast.110), calls=%async_computation.1 | async-start | bytes 16777216 | tf_op jit(solution)/shard_map/all_to_all | solution.py:122
  247.5 4.6 multiply_convert_fusion
  252.1 6.4 %gather_fusion.2 = bf16[32,128,896]{2,1,0:T(8,128)(2,1)} fusion(bf16[16,128,896]{2,1,0:T(8,128)(2,1)} %multiply_convert_fusion, s32[1024]{0:T(1024)S(1)} %pad_clamp_fusion.1), kind=kCustom, calls=%fused_computation.2 | custom fusion | bytes 14680192 | tf_op jit(solution)/shard_map/jit(_take)/gather | solution.py:129
  258.5 0.6 dynamic-slice.4
  259.8 6.8 %broadcast_select_fusion = bf16[32,128,896]{2,1,0:T(8,128)(2,1)} fusion(bf16[32,128,896]{2,1,0:T(8,128)(2,1)} %gather_fusion.2, pred[32]{0:T(512)(128)(4,1)S(1)} %compare_and_fusion), kind=kLoop, calls=%fused_computation.10 | loop fusion | flops 3670016 | bytes 14680096 | tf_op jit(solution)/shard_map/jit(_take)/select_n | solution.py:129
  266.6 93.0 %all-to-all-done.1 = bf16[16,2,128,1024]{3,2,1,0:T(8,128)(2,1)} async-done(((bf16[16,2,128,1024]{3,2,1,0:T(8,128)(2,1)}), bf16[16,2,128,1024]{3,2,1,0:T(8,128)(2,1)}, u32[]{:S(2)}, u32[]{:S(2)}) %all-to-all-start.1) | async-done | bytes 8388640 | tf_op jit(solution)/shard_map/all_to_all | solution.py:122
  359.6 12.3 %convolution_convert_fusion.1 = bf16[896,1024]{1,0:T(8,128)(2,1)S(1)} fusion(bf16[4096,896]{1,0:T(8,128)(2,1)} %bitcast.114, bf16[4096,1024]{1,0:T(8,128)(2,1)} %bitcast.23), kind=kOutput, calls=%fused_computation.34 | convolution fusion | flops 7517110272 | bytes 17563648 | tf_op jit(solution)/shard_map/dot_general | solution.py:19
  371.9 80.4 %fusion = bf16[32,1024]{1,0:T(8,128)(2,1)S(1)} fusion(bf16[896,1024]{1,0:T(8,128)(2,1)S(1)} %convolution_convert_fusion.1), kind=kCustom, calls=%all-reduce-scatter | all-reduce-scatter fusion | flops 1048577 | bytes 1901568
  452.4 2.4 collective-permute-start
  454.8 3.3 collective-permute-start.1
  458.1 4.4 collective-permute-start.2
  462.6 8.0 %collective-permute-start.3 = (bf16[28,1024]{1,0:T(8,128)(2,1)S(1)}, bf16[28,1024]{1,0:T(8,128)(2,1)S(1)}, u32[]{:S(2)}, u32[]{:S(2)}) collective-permute-start(bf16[28,1024]{1,0:T(8,128)(2,1)S(1)} %slice.26), channel_id=1, source_target_pairs={{0,32},{8,40},{16,48},{24,56},{32,64},{40,72},{48,80},{56,88},{64,... | collective-permute-start | bytes 172040
  470.6 2.1 fusion.18
  472.6 0.4 copy.79
  473.1 1.0 reshape.215
  474.5 1.0 reshape.214
  475.5 0.7 concatenate.8
  476.2 0.7 fusion.31
  (57 shorter events, 2.5 us)
Async XLA Ops:
  0.6 51.5 %copy-start.8 = (bf16[896,512]{1,0:T(8,128)(2,1)S(1)}, bf16[896,512]{1,0:T(8,128)(2,1)}, u32[]{:S(2)}) copy-start(bf16[896,512]{1,0:T(8,128)(2,1)} %param.10) | copy-start | bytes 2752516
  0.6 51.5 %copy-start.9 = (bf16[896,512]{1,0:T(8,128)(2,1)S(1)}, bf16[896,512]{1,0:T(8,128)(2,1)}, u32[]{:S(2)}) copy-start(bf16[896,512]{1,0:T(8,128)(2,1)} %param.9) | copy-start | bytes 2752516
  75.2 8.5 %copy-start.6 = (s32[1,8,2]{1,2,0:T(2,128)S(1)}, s32[1,8,2]{1,2,0:T(2,128)}, u32[]{:S(2)}) copy-start(s32[1,8,2]{1,2,0:T(2,128)} %param.11) | copy-start | bytes 196
  75.2 9.2 %copy-start.3 = (bf16[1,512,512]{2,1,0:T(8,128)(2,1)S(1)}, bf16[1,512,512]{2,1,0:T(8,128)(2,1)}, u32[]{:S(2)}) copy-start(bf16[1,512,512]{2,1,0:T(8,128)(2,1)} %param.7) | copy-start | bytes 1572868
  75.2 9.3 %copy-start.4 = (bf16[1,512,512]{2,1,0:T(8,128)(2,1)S(1)}, bf16[1,512,512]{2,1,0:T(8,128)(2,1)}, u32[]{:S(2)}) copy-start(bf16[1,512,512]{2,1,0:T(8,128)(2,1)} %param.13) | copy-start | bytes 1572868
  75.2 100.1 %all-to-all-start = ((bf16[16,2,128,1024]{3,2,1,0:T(8,128)(2,1)}), bf16[16,2,128,1024]{3,2,1,0:T(8,128)(2,1)}, u32[]{:S(2)}, u32[]{:S(2)}) async-start(bf16[16,2,128,1024]{3,2,1,0:T(8,128)(2,1)} %select_select_fusion), calls=%async_computation | async-start | bytes 16777216 | tf_op jit(solution)/shard_map/all_to_all | solution.py:105
  84.5 107.6 %copy-start.1 = (bf16[8,64,4,128]{3,2,1,0:T(4,128)(2,1)}, bf16[8,64,4,128]{3,2,1,0:T(4,128)(2,1)S(1)}, u32[]{:S(2)}) copy-start(bf16[8,64,4,128]{3,2,1,0:T(4,128)(2,1)S(1)} %reshape_squeeze.6) | copy-start | bytes 1572868
  192.1 5.0 %copy-start = (bf16[8,256,2,4,128]{4,1,3,0,2:T(8,128)(2,1)}, bf16[8,256,2,4,128]{4,1,3,0,2:T(8,128)(2,1)S(1)}, u32[]{:S(2)}) copy-start(bf16[8,256,2,4,128]{4,1,3,0,2:T(8,128)(2,1)S(1)} %copy_select_fusion) | copy-start | bytes 12582916
  197.1 1.0 copy-start.2
  237.8 121.8 %all-to-all-start.1 = ((bf16[16,2,128,1024]{3,2,1,0:T(8,128)(2,1)}), bf16[16,2,128,1024]{3,2,1,0:T(8,128)(2,1)}, u32[]{:S(2)}, u32[]{:S(2)}) async-start(bf16[16,2,128,1024]{3,2,1,0:T(8,128)(2,1)} %bitcast.110), calls=%async_computation.1 | async-start | bytes 16777216 | tf_op jit(solution)/shard_map/all_to_all | solution.py:122
  252.1 6.4 %copy-start.7 = (u32[256]{0:T(256)S(1)}, u32[256]{0:T(256)}, u32[]{:S(2)}) copy-start(u32[256]{0:T(256)} %constant.73) | copy-start | bytes 3076
  452.3 21.7 %copy-start.5 = (bf16[8,64,4,128]{3,1,2,0:T(8,128)(2,1)S(1)}, bf16[8,64,4,128]{3,1,2,0:T(8,128)(2,1)}, u32[]{:S(2)}) copy-start(bf16[8,64,4,128]{3,1,2,0:T(8,128)(2,1)} %get-tuple-element.5) | copy-start | bytes 1572868
  452.4 23.1 %collective-permute-start = (bf16[32,1024]{1,0:T(8,128)(2,1)S(1)}, bf16[32,1024]{1,0:T(8,128)(2,1)S(1)}, u32[]{:S(2)}, u32[]{:S(2)}) collective-permute-start(bf16[32,1024]{1,0:T(8,128)(2,1)S(1)} %fusion), channel_id=1, source_target_pairs={{0,8},{8,16},{16,24},{24,32},{32,40},{40,48},{48,56},{56,64},{64,7... | collective-permute-start | bytes 196616
  454.8 20.7 %collective-permute-start.1 = (bf16[32,1024]{1,0:T(8,128)(2,1)S(1)}, bf16[32,1024]{1,0:T(8,128)(2,1)S(1)}, u32[]{:S(2)}, u32[]{:S(2)}) collective-permute-start(bf16[32,1024]{1,0:T(8,128)(2,1)S(1)} %fusion), channel_id=1, source_target_pairs={{0,16},{8,24},{16,32},{24,40},{32,48},{40,56},{48,64},{56,72},{64,... | collective-permute-start | bytes 196616
  458.1 17.4 %collective-permute-start.2 = (bf16[32,1024]{1,0:T(8,128)(2,1)S(1)}, bf16[32,1024]{1,0:T(8,128)(2,1)S(1)}, u32[]{:S(2)}, u32[]{:S(2)}) collective-permute-start(bf16[32,1024]{1,0:T(8,128)(2,1)S(1)} %fusion), channel_id=1, source_target_pairs={{0,24},{8,32},{16,40},{24,48},{32,56},{40,64},{48,72},{56,80},{64,... | collective-permute-start | bytes 196616
  462.6 12.9 %collective-permute-start.3 = (bf16[28,1024]{1,0:T(8,128)(2,1)S(1)}, bf16[28,1024]{1,0:T(8,128)(2,1)S(1)}, u32[]{:S(2)}, u32[]{:S(2)}) collective-permute-start(bf16[28,1024]{1,0:T(8,128)(2,1)S(1)} %slice.26), channel_id=1, source_target_pairs={{0,32},{8,40},{16,48},{24,56},{32,64},{40,72},{48,80},{56,88},{64,... | collective-permute-start | bytes 172040
where the time goes:
time: 478 us; the launch traced here: 477 us
  waiting for transfers between devices  184 us (38%)
  blocking collectives  124 us (26%)
  local copies, waits for them, and re-layouts  70.2 us (15%)
  starting transfers between devices  36.2 us (8%)
  other arithmetic  31.8 us (7%)
  matrix products  29.6 us (6%)
    all_to_all x1, waiting for transfers between devices, local(): lax.all_to_all(grad_slots.reshape(n_ret, capacity, NEIGH_LEN, 2 * feat_wi...  93 us
    all_to_all x1, waiting for transfers between devices, local(): lax.all_to_all(outgoing, 'ret', split_axis=0, concat_axis=0, tiled=True)  90.6 us
    unnamed x1, blocking collectives  80.4 us
    all_gather x1, blocking collectives, local(): lax.all_gather(shard_ids, 'ret', axis=1, tiled=True)  22.1 us
    all_gather x1, blocking collectives, local(): lax.all_gather(row_ids, 'ret', axis=1, tiled=True)  21.5 us
    unnamed x4, starting transfers between devices  18.2 us
    gather x2, local copies, waits for them, and re-layouts, local(): jnp.take(incoming.reshape(n_ret * capacity, NEIGH_LEN, 2 * feat_width), o...  13.9 us
    dot_general x1, matrix products, contract_rows(): lax.dot_general(lhs_rows, rhs_rows, (((0,), (0,)), ((), ())), preferred_e...  12.3 us
  transfers between devices with their start and end apart: 6, of which 2 were waited for; matrix products, arithmetic and copies ran while one was open for 5% of the time, Pallas kernels for 0%

commit v1 on v0

--- a/solution.py
+++ b/solution.py
@@ -70,9 +70,38 @@
     db_dev = enc_states.shape[1] // NEIGH_LEN
     enc_width = enc_states.shape[2]
     context_rows = NEIGHBOURS * NEIGH_LEN
+
+    def draft_the_stacks_all(original):
+        frame_out = lax.axis_size("ret")
+        outcome_arr = lax.axis_index("ret")
+        heap = []
+        view_out, now, q_next = (frame_out, outcome_arr, original.shape[1])
+        for nth in range(view_out):
+            heap.append((nth, (nth + 1) % view_out))
+        column = []
+        for nth in range(view_out):
+            column.append((nth, (nth - 1) % view_out))
+        big = jnp.zeros(
+            (*original.shape[:1], view_out * q_next, *original.shape[2:]), original.dtype
+        )
+        parts_out = found_now = original
+        ready = view_out // 2
+        big = lax.dynamic_update_slice_in_dim(big, original, now * q_next, axis=1)
+        for dev_i in range(1, ready + 1):
+            parts_out = lax.ppermute(parts_out, "ret", heap)
+            big = lax.dynamic_update_slice_in_dim(
+                big, parts_out, (now - dev_i) % view_out * q_next, axis=1
+            )
+            if dev_i < view_out - ready:
+                found_now = lax.ppermute(found_now, "ret", column)
+                big = lax.dynamic_update_slice_in_dim(
+                    big, found_now, (now + dev_i) % view_out * q_next, axis=1
+                )
+        return big
+
     every_shard, every_row = (
         lax.all_gather(shard_ids, "ret", axis=1, tiled=True),
-        lax.all_gather(row_ids, "ret", axis=1, tiled=True),
+        draft_the_stacks_all(row_ids),
     )
     req_shard = every_shard.reshape(n_ret, request_count)
     req_row = every_row.reshape(n_ret, request_count)

time: 478 us -> 514 us (1.075)
  starting transfers between devices: 36.2 us -> 66.5 us
  blocking collectives: 124 us -> 102 us
  waiting for transfers between devices: 184 us -> 204 us
    all_gather x1 -> x0, blocking collectives: 21.5 us -> none  [local(): lax.all_gather(row_ids, 'ret', axis=1, tiled=True)]
    ppermute x0 -> x15, waiting for transfers between devices: none -> 19.9 us  [the longest x7 10.4 us: draft_the_stacks_all(): found_now = lax.ppermute(found_now, 'ret', column)]
    ppermute x0 -> x15, starting transfers between devices: none -> 19.5 us  [the longest x8 18.4 us: draft_the_stacks_all(): parts_out = lax.ppermute(parts_out, 'ret', heap)]
    all_to_all x1, starting transfers between devices: 8.48 us -> 19 us  [local(): lax.all_to_all(outgoing, 'ret', split_axis=0, concat_axis=0, tiled=True)]
  transfers between devices with their start and end apart: 6 -> 21, of which waited for: 2 -> 14; matrix products, arithmetic and copies ran while one was open for 5% -> 8% of each run, Pallas kernels for 0% -> 0%
where the time goes in v1:
time: 514 us; the launch traced here: 513 us
  waiting for transfers between devices  204 us (40%)
  blocking collectives  102 us (20%)
  local copies, waits for them, and re-layouts  75.3 us (15%)
  starting transfers between devices  66.5 us (13%)
  matrix products  32.9 us (6%)
  other arithmetic  30.4 us (6%)
    all_to_all x1, waiting for transfers between devices, local(): lax.all_to_all(grad_slots.reshape(n_ret, capacity, NEIGH_LEN, 2 * feat_wi...  96.2 us
    all_to_all x1, waiting for transfers between devices, local(): lax.all_to_all(outgoing, 'ret', split_axis=0, concat_axis=0, tiled=True)  87.9 us
    unnamed x1, blocking collectives  79 us
    all_gather x1, blocking collectives, local(): lax.all_gather(shard_ids, 'ret', axis=1, tiled=True)  22.9 us
    unnamed x4, starting transfers between devices  20 us
    all_to_all x1, starting transfers between devices, local(): lax.all_to_all(outgoing, 'ret', split_axis=0, concat_axis=0, tiled=True)  19 us
    ppermute x8, starting transfers between devices, draft_the_stacks_all(): parts_out = lax.ppermute(parts_out, 'ret', heap)  18.4 us
    gather x2, local copies, waits for them, and re-layouts, local(): jnp.take(incoming.reshape(n_ret * capacity, NEIGH_LEN, 2 * feat_width), o...  13.9 us
  transfers between devices with their start and end apart: 21, of which 14 were waited for; matrix products, arithmetic and copies ran while one was open for 8% of the time, Pallas kernels for 0%

profile of v1, /device:TPU:76, one launch (start us, length us, event | category | flops | bytes accessed | tf_op | source)
XLA Modules:
  0.0 512.5 jit_solution(11346525840622739190)
XLA Ops:
  4.3 22.9 %all_gather.3 = s32[1,128,2]{2,0,1:T(1,128)S(1)} all-gather(s32[1,8,2]{2,0,1:T(1,128)S(1)} %copy.112), channel_id=1, replica_groups=mesh['dp'=2,'ret'=16,'ctx'=8] {'ret'}, dimensions={1}, use_global_device_ids=true | all-gather | bytes 1088 | tf_op jit(solution)/shard_map/all_gather | solution.py:103
  29.0 2.8 fusion.1
  32.1 8.4 %convolution_convert_fusion = bf16[2048,1024]{1,0:T(8,128)(2,1)} fusion(bf16[1,2048,896]{2,1,0:T(8,128)(2,1)} %param.8, f32[2048]{0:T(1024)S(1)} %get-tuple-element.9, bf16[896,512]{1,0:T(8,128)(2,1)S(1)} %copy-done.11, bf16[896,512]{1,0:T(8,128)(2,1)S(1)} %copy-done.12), kind=kOutput, calls=%fused_computation.13 | convolution fusion | flops 3769368576 | bytes 9707520 | tf_op jit(solution)/shard_map/dot_general | solution.py:127
  40.7 1.8 collective-permute-start.2
  42.7 1.5 collective-permute-done.2
  44.4 1.8 collective-permute-done.3
  46.2 4.1 collective-permute-start.4
  51.7 2.2 collective-permute-done.5
  54.0 2.2 collective-permute-start.6
  57.7 2.1 collective-permute-done.7
  59.9 2.2 collective-permute-start.8
  63.5 2.1 collective-permute-done.9
  65.8 2.4 collective-permute-start.10
  69.5 2.2 collective-permute-done.11
  71.8 2.2 collective-permute-start.12
  74.0 1.4 collective-permute-done.12
  75.5 2.2 collective-permute-start.14
  79.6 7.1 %gather_fusion = bf16[32,128,1024]{2,1,0:T(8,128)(2,1)} fusion(bf16[16,128,1024]{2,1,0:T(8,128)(2,1)} %bitcast.111, s32[1024]{0:T(1024)S(1)} %pad_clamp_fusion.1), kind=kCustom, calls=%fused_computation | custom fusion | bytes 16777344 | tf_op jit(solution)/shard_map/jit(_take)/gather | solution.py:131
  86.7 7.6 %select_select_fusion = bf16[16,2,128,1024]{3,2,1,0:T(8,128)(2,1)} fusion(bf16[16,2,128,1024]{3,2,1,0:T(8,128)(2,1)} %bitcast.110, pred[16,2]{1,0:T(8,128)(4,1)S(1)} %copy.130, pred[16,2]{1,0:T(8,128)(4,1)S(1)} %copy.113), kind=kLoop, calls=%fused_computation.4 | loop fusion | flops 8388608 | bytes 16777280 | tf_op jit(solution)/shard_map/jit(_where)/select_n | solution.py:132
  94.3 19.0 %all-to-all-start = ((bf16[16,2,128,1024]{3,2,1,0:T(8,128)(2,1)}), bf16[16,2,128,1024]{3,2,1,0:T(8,128)(2,1)}, u32[]{:S(2)}, u32[]{:S(2)}) async-start(bf16[16,2,128,1024]{3,2,1,0:T(8,128)(2,1)} %select_select_fusion), calls=%async_computation | async-start | bytes 16777216 | tf_op jit(solution)/shard_map/all_to_all | solution.py:134
  114.4 87.9 %all-to-all-done = bf16[16,2,128,1024]{3,2,1,0:T(8,128)(2,1)} async-done(((bf16[16,2,128,1024]{3,2,1,0:T(8,128)(2,1)}), bf16[16,2,128,1024]{3,2,1,0:T(8,128)(2,1)}, u32[]{:S(2)}, u32[]{:S(2)}) %all-to-all-start) | async-done | bytes 8388640 | tf_op jit(solution)/shard_map/all_to_all | solution.py:134
  202.3 6.2 %gather_fusion.1 = bf16[16,128,1024]{2,1,0:T(8,128)(2,1)} fusion(bf16[32,128,1024]{2,1,0:T(8,128)(2,1)} %bitcast.6, s32[1024]{0:T(1024)S(1)} %pad_clamp_fusion), kind=kCustom, calls=%fused_computation.1 | custom fusion | bytes 8388672 | tf_op jit(solution)/shard_map/jit(_take)/gather | solution.py:135
  208.4 7.7 %reshape.255 = bf16[8,256,2,4,128]{4,3,2,1,0:T(4,128)(2,1)} reshape(bf16[16,128,1024]{2,1,0:T(8,128)(2,1)} %gather_fusion.1) | data formatting | bytes 8388608 | tf_op jit(solution)/shard_map/jit(_take)/gather | solution.py:135
  216.1 2.9 copy_select_fusion
  219.0 2.0 copy-done
  223.4 2.5 convert_bitcast_fusion
  225.9 3.3 copy.144
  229.2 2.2 reshape.218
  231.4 3.8 multiply_reduce_fusion
  235.7 1.9 fusion.7
  238.4 2.9 copy.142
  241.3 4.2 reshape.217
  245.5 3.9 pad_maximum_fusion
  249.4 6.8 %copy.145 = bf16[16,128,1024]{2,1,0:T(8,128)(2,1)} copy(bf16[16,128,1024]{1,0,2:T(8,128)(2,1)} %pad_maximum_fusion) | data formatting | bytes 8388608 | tf_op jit(solution)/shard_map/concatenate | solution.py:142
  256.2 4.3 broadcast.189
  260.5 10.9 %scatter_fusion = bf16[32,128,1024]{2,1,0:T(8,128)(2,1)} fusion(bf16[32,128,1024]{2,1,0:T(8,128)(2,1)} %broadcast.189, s32[16]{0:T(128)S(1)} %fusion.27, bf16[16,128,1024]{2,1,0:T(8,128)(2,1)} %copy.145), kind=kCustom, calls=%fused_computation.3 | custom fusion | bytes 12582976 | tf_op jit(solution)/shard_map/scatter | solution.py:150
  271.4 8.1 %all-to-all-start.1 = ((bf16[16,2,128,1024]{3,2,1,0:T(8,128)(2,1)}), bf16[16,2,128,1024]{3,2,1,0:T(8,128)(2,1)}, u32[]{:S(2)}, u32[]{:S(2)}) async-start(bf16[16,2,128,1024]{3,2,1,0:T(8,128)(2,1)} %bitcast.109), calls=%async_computation.1 | async-start | bytes 16777216 | tf_op jit(solution)/shard_map/all_to_all | solution.py:151
  280.7 4.6 multiply_convert_fusion
  285.4 6.4 %gather_fusion.2 = bf16[32,128,896]{2,1,0:T(8,128)(2,1)} fusion(bf16[16,128,896]{2,1,0:T(8,128)(2,1)} %multiply_convert_fusion, s32[1024]{0:T(1024)S(1)} %pad_clamp_fusion.1), kind=kCustom, calls=%fused_computation.2 | custom fusion | bytes 14680192 | tf_op jit(solution)/shard_map/jit(_take)/gather | solution.py:158
  291.8 6.8 %broadcast_select_fusion = bf16[32,128,896]{2,1,0:T(8,128)(2,1)} fusion(bf16[32,128,896]{2,1,0:T(8,128)(2,1)} %gather_fusion.2, pred[32]{0:T(512)(128)(4,1)S(1)} %compare_and_fusion), kind=kLoop, calls=%fused_computation.10 | loop fusion | flops 3670016 | bytes 14680096 | tf_op jit(solution)/shard_map/jit(_take)/select_n | solution.py:158
  298.6 96.2 %all-to-all-done.1 = bf16[16,2,128,1024]{3,2,1,0:T(8,128)(2,1)} async-done(((bf16[16,2,128,1024]{3,2,1,0:T(8,128)(2,1)}), bf16[16,2,128,1024]{3,2,1,0:T(8,128)(2,1)}, u32[]{:S(2)}, u32[]{:S(2)}) %all-to-all-start.1) | async-done | bytes 8388640 | tf_op jit(solution)/shard_map/all_to_all | solution.py:151
  394.8 12.3 %convolution_convert_fusion.1 = bf16[896,1024]{1,0:T(8,128)(2,1)S(1)} fusion(bf16[4096,896]{1,0:T(8,128)(2,1)} %bitcast.113, bf16[4096,1024]{1,0:T(8,128)(2,1)} %bitcast.23), kind=kOutput, calls=%fused_computation.34 | convolution fusion | flops 7517110272 | bytes 17563648 | tf_op jit(solution)/shard_map/dot_general | solution.py:19
  407.2 79.0 %fusion = bf16[32,1024]{1,0:T(8,128)(2,1)S(1)} fusion(bf16[896,1024]{1,0:T(8,128)(2,1)S(1)} %convolution_convert_fusion.1), kind=kCustom, calls=%all-reduce-scatter | all-reduce-scatter fusion | flops 1048577 | bytes 1901568
  486.2 4.4 collective-permute-start.15
  490.6 1.9 collective-permute-start.16
  492.5 5.5 %collective-permute-start.17 = (bf16[32,1024]{1,0:T(8,128)(2,1)S(1)}, bf16[32,1024]{1,0:T(8,128)(2,1)S(1)}, u32[]{:S(2)}, u32[]{:S(2)}) collective-permute-start(bf16[32,1024]{1,0:T(8,128)(2,1)S(1)} %fusion), channel_id=1, source_target_pairs={{0,24},{8,32},{16,40},{24,48},{32,56},{40,64},{48,72},{56,80},{64,... | collective-permute-start | bytes 196616
  498.0 8.2 %collective-permute-start.18 = (bf16[28,1024]{1,0:T(8,128)(2,1)S(1)}, bf16[28,1024]{1,0:T(8,128)(2,1)S(1)}, u32[]{:S(2)}, u32[]{:S(2)}) collective-permute-start(bf16[28,1024]{1,0:T(8,128)(2,1)S(1)} %slice.26), channel_id=1, source_target_pairs={{0,32},{8,40},{16,48},{24,56},{32,64},{40,72},{48,80},{56,88},{64,... | collective-permute-start | bytes 172040
  506.2 2.1 fusion.18
  (127 shorter events, 23.8 us)
Async XLA Ops:
  0.6 31.5 %copy-start.11 = (bf16[896,512]{1,0:T(8,128)(2,1)S(1)}, bf16[896,512]{1,0:T(8,128)(2,1)}, u32[]{:S(2)}) copy-start(bf16[896,512]{1,0:T(8,128)(2,1)} %param.10) | copy-start | bytes 2752516
  0.6 31.5 %copy-start.12 = (bf16[896,512]{1,0:T(8,128)(2,1)S(1)}, bf16[896,512]{1,0:T(8,128)(2,1)}, u32[]{:S(2)}) copy-start(bf16[896,512]{1,0:T(8,128)(2,1)} %param.9) | copy-start | bytes 2752516
  0.7 39.9 %collective-permute-start = (s32[1,8,2]{1,2,0:T(2,128)}, s32[1,8,2]{1,2,0:T(2,128)S(1)}, u32[]{:S(2)}, u32[]{:S(2)}) collective-permute-start(s32[1,8,2]{1,2,0:T(2,128)} %param.12), channel_id=1, source_target_pairs={{0,8},{8,16},{16,24},{24,32},{32,40},{40,48},{48,56},{56,64},{64,7... | collective-permute-start | bytes 200 | tf_op jit(solution)/shard_map/ppermute | solution.py:91
  1.9 38.7 %collective-permute-start.1 = (s32[1,8,2]{1,2,0:T(2,128)}, s32[1,8,2]{1,2,0:T(2,128)S(1)}, u32[]{:S(2)}, u32[]{:S(2)}) collective-permute-start(s32[1,8,2]{1,2,0:T(2,128)} %param.12), channel_id=1, source_target_pairs={{0,120},{8,0},{16,8},{24,16},{32,24},{40,32},{48,40},{56,48},{64,5... | collective-permute-start | bytes 200 | tf_op jit(solution)/shard_map/ppermute | solution.py:96
  40.7 3.6 collective-permute-start.2
  42.5 3.6 collective-permute-start.3
  46.2 5.4 %collective-permute-start.4 = (s32[1,8,2]{1,2,0:T(2,128)S(1)}, s32[1,8,2]{1,2,0:T(2,128)S(1)}, u32[]{:S(2)}, u32[]{:S(2)}) collective-permute-start(s32[1,8,2]{1,2,0:T(2,128)S(1)} %collective-permute-done.2), channel_id=1, source_target_pairs={{0,8},{8,16},{16,24},{24,32},{32,40},{40,48},{48,56},{56,64},{64,7... | collective-permute-start | bytes 200 | tf_op jit(solution)/shard_map/ppermute | solution.py:91
  50.4 3.6 collective-permute-start.5
  54.0 3.6 collective-permute-start.6
  56.2 3.6 collective-permute-start.7
  59.9 3.6 collective-permute-start.8
  62.1 3.6 collective-permute-start.9
  65.8 3.7 collective-permute-start.10
  68.1 3.6 collective-permute-start.11
  71.8 3.6 collective-permute-start.12
  74.0 3.7 collective-permute-start.13
  75.5 3.6 collective-permute-start.14
  94.3 19.0 %copy-start.9 = (s32[1,8,2]{1,2,0:T(2,128)S(1)}, s32[1,8,2]{1,2,0:T(2,128)}, u32[]{:S(2)}) copy-start(s32[1,8,2]{1,2,0:T(2,128)} %param.11) | copy-start | bytes 196
  94.3 19.7 %copy-start.5 = (bf16[1,512,512]{2,1,0:T(8,128)(2,1)S(1)}, bf16[1,512,512]{2,1,0:T(8,128)(2,1)}, u32[]{:S(2)}) copy-start(bf16[1,512,512]{2,1,0:T(8,128)(2,1)} %param.7) | copy-start | bytes 1572868
  94.3 19.8 %copy-start.6 = (bf16[1,512,512]{2,1,0:T(8,128)(2,1)S(1)}, bf16[1,512,512]{2,1,0:T(8,128)(2,1)}, u32[]{:S(2)}) copy-start(bf16[1,512,512]{2,1,0:T(8,128)(2,1)} %param.13) | copy-start | bytes 1572868
  94.3 108.0 %all-to-all-start = ((bf16[16,2,128,1024]{3,2,1,0:T(8,128)(2,1)}), bf16[16,2,128,1024]{3,2,1,0:T(8,128)(2,1)}, u32[]{:S(2)}, u32[]{:S(2)}) async-start(bf16[16,2,128,1024]{3,2,1,0:T(8,128)(2,1)} %select_select_fusion), calls=%async_computation | async-start | bytes 16777216 | tf_op jit(solution)/shard_map/all_to_all | solution.py:134
  114.1 104.9 %copy-start.3 = (bf16[8,64,4,128]{3,2,1,0:T(4,128)(2,1)}, bf16[8,64,4,128]{3,2,1,0:T(4,128)(2,1)S(1)}, u32[]{:S(2)}) copy-start(bf16[8,64,4,128]{3,2,1,0:T(4,128)(2,1)S(1)} %reshape_squeeze.6) | copy-start | bytes 1572868
  114.2 117.2 %copy-start.8 = (bf16[8,64,4,128]{3,2,1,0:T(4,128)(2,1)}, bf16[8,64,4,128]{3,2,1,0:T(4,128)(2,1)S(1)}, u32[]{:S(2)}) copy-start(bf16[8,64,4,128]{3,2,1,0:T(4,128)(2,1)S(1)} %reshape_squeeze.7) | copy-start | bytes 1572868
  219.0 2.1 copy-start
  222.0 1.3 copy-start.13
  231.4 3.8 copy-start.1
  231.4 4.3 copy-start.14
  235.7 2.0 copy-start.4
  241.3 4.2 copy-start.2
  271.4 8.1 %copy-start.10 = (u32[256]{0:T(256)S(1)}, u32[256]{0:T(256)}, u32[]{:S(2)}) copy-start(u32[256]{0:T(256)} %constant.173) | copy-start | bytes 3076
  271.4 123.4 %all-to-all-start.1 = ((bf16[16,2,128,1024]{3,2,1,0:T(8,128)(2,1)}), bf16[16,2,128,1024]{3,2,1,0:T(8,128)(2,1)}, u32[]{:S(2)}, u32[]{:S(2)}) async-start(bf16[16,2,128,1024]{3,2,1,0:T(8,128)(2,1)} %bitcast.109), calls=%async_computation.1 | async-start | bytes 16777216 | tf_op jit(solution)/shard_map/all_to_all | solution.py:151
  486.2 23.5 %copy-start.7 = (bf16[8,64,4,128]{3,1,2,0:T(8,128)(2,1)S(1)}, bf16[8,64,4,128]{3,1,2,0:T(8,128)(2,1)}, u32[]{:S(2)}) copy-start(bf16[8,64,4,128]{3,1,2,0:T(8,128)(2,1)} %get-tuple-element.5) | copy-start | bytes 1572868
  486.2 24.9 %collective-permute-start.15 = (bf16[32,1024]{1,0:T(8,128)(2,1)S(1)}, bf16[32,1024]{1,0:T(8,128)(2,1)S(1)}, u32[]{:S(2)}, u32[]{:S(2)}) collective-permute-start(bf16[32,1024]{1,0:T(8,128)(2,1)S(1)} %fusion), channel_id=1, source_target_pairs={{0,8},{8,16},{16,24},{24,32},{32,40},{40,48},{48,56},{56,64},{64,7... | collective-permute-start | bytes 196616
  490.6 20.5 %collective-permute-start.16 = (bf16[32,1024]{1,0:T(8,128)(2,1)S(1)}, bf16[32,1024]{1,0:T(8,128)(2,1)S(1)}, u32[]{:S(2)}, u32[]{:S(2)}) collective-permute-start(bf16[32,1024]{1,0:T(8,128)(2,1)S(1)} %fusion), channel_id=1, source_target_pairs={{0,16},{8,24},{16,32},{24,40},{32,48},{40,56},{48,64},{56,72},{64,... | collective-permute-start | bytes 196616
  492.5 18.6 %collective-permute-start.17 = (bf16[32,1024]{1,0:T(8,128)(2,1)S(1)}, bf16[32,1024]{1,0:T(8,128)(2,1)S(1)}, u32[]{:S(2)}, u32[]{:S(2)}) collective-permute-start(bf16[32,1024]{1,0:T(8,128)(2,1)S(1)} %fusion), channel_id=1, source_target_pairs={{0,24},{8,32},{16,40},{24,48},{32,56},{40,64},{48,72},{56,80},{64,... | collective-permute-start | bytes 196616
  498.0 13.1 %collective-permute-start.18 = (bf16[28,1024]{1,0:T(8,128)(2,1)S(1)}, bf16[28,1024]{1,0:T(8,128)(2,1)S(1)}, u32[]{:S(2)}, u32[]{:S(2)}) collective-permute-start(bf16[28,1024]{1,0:T(8,128)(2,1)S(1)} %slice.26), channel_id=1, source_target_pairs={{0,32},{8,40},{16,48},{24,56},{32,64},{40,72},{48,80},{56,88},{64,... | collective-permute-start | bytes 172040
